TPU v7x, 32 devices: a 4x4x1 block of a 4x4x8 slice. The times are simulated.
32 devices in a mesh: dp: 1 (over z), tp: 4 (over y), ep: 8 (over x, core).
Axes of the slice: x: 4, y: 4, z: 1, core: 2. Of those that a mesh axis runs over, the one named last changes fastest.
The devices are a block of a 4x4x8 slice.
Arguments:
- tokens: bfloat16 [8192, 2048], P(('dp', 'ep'))
- expert_ids: int32 [8192, 8], P(('dp', 'ep'))
- norm_gain: bfloat16 [2048], replicated
- router_w: bfloat16 [2048, 64], replicated
- w_gate: bfloat16 [64, 2048, 1024], P('ep', None, 'tp')
- w_up: bfloat16 [64, 2048, 1024], P('ep', None, 'tp')
- w_down: bfloat16 [64, 1024, 2048], P('ep', 'tp')
Outputs:
- output: bfloat16 [8192, 2048], P(('dp', 'ep'))
All inputs are finite; a program needn't handle non-finite values.
Results may differ from a plain program's by a relative error of at most 0.0119738.
Values are sent between devices in bfloat16 or wider.
A program may use at most 768 MiB of HBM per device.

v0:
```python
import jax
import jax.numpy as jnp
from jax import lax
from jax.sharding import PartitionSpec as P

NORM_EPS = 1e-5


def route_local(tokens, expert_ids, norm_gain, router_w):
    num_tok, top_k = expert_ids.shape
    num_exp = router_w.shape[1]
    slot_cap = 2 * top_k * num_tok // num_exp
    tok_f32 = tokens.astype(jnp.float32)
    inv_rms = lax.rsqrt(jnp.mean(tok_f32 * tok_f32, axis=-1, keepdims=True) + NORM_EPS)
    normed = (tok_f32 * inv_rms * norm_gain.astype(jnp.float32)).astype(jnp.bfloat16)
    logits = jnp.dot(normed, router_w, preferred_element_type=jnp.float32)
    gates = jax.nn.softmax(jnp.take_along_axis(logits, expert_ids, axis=1), axis=-1)
    flat_ids = expert_ids.reshape(-1)
    onehot = (flat_ids[:, None] == jnp.arange(num_exp, dtype=jnp.int32)[None, :]).astype(jnp.int32)
    slot_ids = jnp.sum(jnp.cumsum(onehot, axis=0) * onehot, axis=1) - 1
    dest_pos = flat_ids * slot_cap + slot_ids
    row_tok = jnp.arange(num_tok * top_k, dtype=jnp.int32) // top_k
    src_rows = jnp.zeros((num_exp * slot_cap,), jnp.int32).at[dest_pos].set(row_tok)
    return normed, gates, src_rows, dest_pos


def expert_ffn(rows, w_gate, w_up, w_down):
    gate_act = jnp.einsum('ecd,edf->ecf', rows, w_gate, preferred_element_type=jnp.float32)
    up_act = jnp.einsum('ecd,edf->ecf', rows, w_up, preferred_element_type=jnp.float32)
    hidden = (jax.nn.silu(gate_act) * up_act).astype(jnp.bfloat16)
    return jnp.einsum('ecf,efd->ecd', hidden, w_down, preferred_element_type=jnp.float32).astype(jnp.bfloat16)


def solution(mesh):
    ep_size = mesh.shape['ep']
    tok_spec = P(('dp', 'ep'), None)

    def local_block(tokens, expert_ids, norm_gain, router_w, w_gate, w_up, w_down):
        num_tok, model_dim = tokens.shape
        top_k = expert_ids.shape[1]
        num_exp = router_w.shape[1]
        local_exp = num_exp // ep_size
        slot_cap = 2 * top_k * num_tok // num_exp
        normed, gates, src_rows, dest_pos = route_local(tokens, expert_ids, norm_gain, router_w)
        send_buf = normed[src_rows].reshape(ep_size, local_exp, slot_cap, model_dim)
        recv_buf = lax.all_to_all(send_buf, 'ep', 0, 2, tiled=True)
        recv_buf = recv_buf.reshape(local_exp, ep_size * slot_cap, model_dim)
        part_out = expert_ffn(recv_buf, w_gate, w_up, w_down)
        full_out = lax.psum(part_out, 'tp')
        full_out = full_out.reshape(1, local_exp, ep_size * slot_cap, model_dim)
        back_buf = lax.all_to_all(full_out, 'ep', 2, 0, tiled=True)
        back_buf = back_buf.reshape(num_exp * slot_cap, model_dim)
        picked = back_buf[dest_pos].reshape(num_tok, top_k, model_dim).astype(jnp.float32)
        mixed = jnp.sum(gates[:, :, None] * picked, axis=1)
        return (tokens.astype(jnp.float32) + mixed).astype(jnp.bfloat16)

    return jax.shard_map(local_block, mesh=mesh, in_specs=(tok_spec, tok_spec, P(None), P(None, None), P('ep', None, 'tp'), P('ep', None, 'tp'), P('ep', 'tp', None)), out_specs=tok_spec, check_vma=False)
```

profile of v0, /device:TPU:97, one launch (start us, length us, event | category | flops | bytes accessed | tf_op | source)
XLA Modules:
  0.0 3285.4 jit_solution(9832182584285457979)
XLA Ops:
  6.5 0.0 copy-start
  6.6 0.0 all-reduce.2.cloned.1.call-start
  6.6 0.8 broadcast_multiply_fusion
  7.4 0.9 copy.36
  8.3 0.3 eq.29
  8.6 0.3 eq.25
  8.8 3.1 fusion.1
  11.9 0.7 convert_element_type.31
  12.6 0.2 copy.35
  12.8 0.3 mul.61
  13.1 1.6 fusion.10
  14.7 34.0 %reduce-window.6 = s32[64,64,128]{2,1,0:T(8,128)S(1)} reduce-window(s32[64,64,128]{2,1,0:T(8,128)} %fusion.10, s32[]{:T(128)} %constant.31.clone.1), window={size=1x1x128 pad=0_0x0_0x127_0}, to_apply=%region_3.4 | reduce-window | flops 66584576 | bytes 4194308 | tf_op jit(solution)/shard_map/reduce-window
  48.7 1.7 slice_reduce_fusion
  50.4 0.2 reduce-window.9
  50.6 0.7 broadcast_add_fusion
  51.3 1.8 fusion.9
  53.1 0.1 compare_select_fusion
  53.2 0.0 copy-start.3
  53.2 0.6 copy-done.3
  53.8 30.5 scatter_custom_fusion
  84.3 5.2 fusion.3
  89.5 124.1 %gather_fusion = bf16[16384,2048]{1,0:T(8,128)(2,1)} fusion(bf16[1024,2048]{1,0:T(8,128)(2,1)} %fusion.3, s32[16384]{0:T(1024)S(1)} %fusion.11), kind=kCustom, calls=%fused_computation | custom fusion | bytes 134283264 | tf_op jit(solution)/shard_map/gather | solution.py:45
  213.6 742.9 %all_to_all.30 = bf16[8,8,256,2048]{3,2,1,0:T(8,128)(2,1)} all-to-all(bf16[8,8,256,2048]{3,2,1,0:T(8,128)(2,1)} %bitcast.4), channel_id=1, replica_groups=mesh['dp'=1,'tp'=4,'ep'=8] {'ep'}, dimensions={0} | all-to-all | bytes 134217728 | tf_op jit(solution)/shard_map/all_to_all | solution.py:46
  956.5 44.0 %copy.38 = bf16[1,8,8,256,2048]{4,3,2,1,0:T(8,128)(2,1)} copy(bf16[1,8,8,256,2048]{4,3,1,2,0:T(8,128)(2,1)} %bitcast.6) | data formatting | bytes 134217728 | tf_op jit(solution)/shard_map/all_to_all | solution.py:46
  1000.6 33.1 %fusion.22 = f32[8,2048,256]{2,1,0:T(8,128)} fusion(bf16[8,2048,2048]{2,1,0:T(8,128)(2,1)} %bitcast.7, bf16[8,2048,256]{2,1,0:T(8,128)(2,1)} %param.11), kind=kOutput, calls=%fused_computation.50 | convolution fusion | flops 17179869184 | bytes 92274688 | tf_op jit(solution)/shard_map/ecd,edf->ecf/dot_general | solution.py:28
  1033.6 35.6 %multiply_convert_fusion.4 = bf16[8,2048,256]{2,1,0:T(8,128)(2,1)} fusion(f32[8,2048,256]{2,1,0:T(8,128)} %fusion.22, bf16[8,2048,2048]{2,1,0:T(8,128)(2,1)} %bitcast.7, bf16[8,2048,256]{2,1,0:T(8,128)(2,1)} %param.12), kind=kOutput, calls=%fused_computation.7.clone.clone.1 | convolution fusion | flops 17205035008 | bytes 100663296 | tf_op jit(solution)/shard_map/ecd,edf->ecf/dot_general | solution.py:29
  1069.2 30.0 convert_bitcast_fusion
  1099.2 0.1 all-reduce.2.cloned.1.call-update
  1099.3 1100.6 %all-reduce.2.cloned.1.call-done = bf16[1,8,2048,2048]{3,2,1,0:T(8,128)(2,1)} async-done(((bf16[1,8,2048,2048]{3,2,1,0:T(8,128)(2,1)}), bf16[1,8,2048,2048]{3,2,1,0:T(8,128)(2,1)}) %all-reduce.2.cloned.1.call-update) | async-done | bytes 67108880 | tf_op jit(solution)/shard_map/psum | solution.py:49
  2199.9 57.2 %copy.39 = bf16[1,8,2048,2048]{3,1,0,2:T(8,128)(2,1)} copy(bf16[1,8,2048,2048]{3,2,1,0:T(8,128)(2,1)} %all-reduce.2.cloned.1.call-done) | data formatting | bytes 134217728 | tf_op jit(solution)/shard_map/psum | solution.py:49
  2257.1 0.0 copy-start.1
  2257.1 10.8 all-to-all-start.1
  2267.9 0.0 copy-done.1
  2267.9 0.2 copy.32
  2268.1 0.3 reshape.129
  2268.3 0.0 copy-done
  2268.4 3.6 fusion.21
  2271.9 0.0 copy-start.2
  2271.9 0.0 copy-start.4
  2272.0 65.5 %gather_fusion.2 = f32[8192]{0:T(1024)S(1)} fusion(f32[1024,64]{0,1:T(8,128)S(1)} %fusion.21, s32[8192]{0:T(1024)S(1)} %reshape.129), kind=kCustom, calls=%fused_computation.2 | custom fusion | bytes 131072 | tf_op jit(solution)/shard_map/jit(take_along_axis)/gather | solution.py:17
  2337.5 0.3 reshape.132
  2337.8 0.2 copy.33
  2338.0 0.0 copy-done.2
  2338.1 0.2 copy.34
  2338.3 0.0 copy-done.4
  2338.3 652.4 %all-to-all-done.1 = bf16[1,8,2048,2048]{3,1,0,2:T(8,128)(2,1)} async-done(((bf16[1,8,2048,2048]{3,1,0,2:T(8,128)(2,1)}), bf16[1,8,2048,2048]{3,1,0,2:T(8,128)(2,1)}, u32[]{:S(2)}, u32[]{:S(2)}) %all-to-all-start.1) | async-done | bytes 67108896 | tf_op jit(solution)/shard_map/all_to_all | solution.py:51
  2990.7 57.3 %copy.40 = bf16[1,8,8,256,2048]{4,3,1,2,0:T(8,128)(2,1)} copy(bf16[1,8,8,256,2048]{4,1,3,2,0:T(8,128)(2,1)} %bitcast.9) | data formatting | bytes 134217728 | tf_op jit(solution)/shard_map/all_to_all | solution.py:51
  3047.9 191.2 %gather_fusion.1 = bf16[8192,2048]{1,0:T(8,128)(2,1)} fusion(bf16[16384,2048]{1,0:T(8,128)(2,1)} %bitcast.11, s32[8192]{0:T(1024)S(1)} %broadcast_clamp_fusion), kind=kCustom, calls=%fused_computation.1 | custom fusion | bytes 67141632 | tf_op jit(solution)/shard_map/gather | solution.py:53
  3239.1 31.1 fusion
  3270.2 8.3 fusion.4
  (9 shorter events, 0.1 us)
Async XLA Ops:
  6.5 2261.8 %copy-start = (bf16[2048,64]{0,1:T(8,128)(2,1)S(1)}, bf16[2048,64]{0,1:T(8,128)(2,1)}, u32[]{:S(2)}) copy-start(bf16[2048,64]{0,1:T(8,128)(2,1)} %param.10) | copy-start | bytes 786436
  6.6 2193.3 %all-reduce.2.cloned.1.call-start = ((), (), s32[]{:S(2)}) async-start(), calls=%async_computation.2 | async-start | bytes 134217728 | tf_op jit(solution)/shard_map/psum | solution.py:49
  53.2 0.6 copy-start.3
  2257.1 10.8 copy-start.1
  2257.1 733.6 %all-to-all-start.1 = ((bf16[1,8,2048,2048]{3,1,0,2:T(8,128)(2,1)}), bf16[1,8,2048,2048]{3,1,0,2:T(8,128)(2,1)}, u32[]{:S(2)}, u32[]{:S(2)}) async-start(bf16[1,8,2048,2048]{3,1,0,2:T(8,128)(2,1)} %copy.39), calls=%async_computation.1 | async-start | bytes 134217728 | tf_op jit(solution)/shard_map/all_to_all | solution.py:51
  2271.9 66.0 %copy-start.2 = (s32[1024,8]{0,1:T(8,128)S(1)}, s32[1024,8]{0,1:T(8,128)}, u32[]{:S(2)}) copy-start(s32[1024,8]{0,1:T(8,128)} %param.8) | copy-start | bytes 98308
  2271.9 66.3 %copy-start.4 = (s32[8192,1]{0,1:T(1,128)S(1)}, s32[8192,1]{0,1:T(1,128)}, u32[]{:S(2)}) copy-start(s32[8192,1]{0,1:T(1,128)} %copy-done.3) | copy-start | bytes 98308
Sparse Core Ops, SparseCore 0:
  1099.4 1100.4 all-reduce.1
where the time goes:
time: 3290 us
  waiting for transfers between devices  1750 us (53%)
  blocking collectives  743 us (23%)
  local copies, waits for them, and re-layouts  575 us (17%)
  matrix products  102 us (3%)
  other arithmetic  87.6 us (3%)
    psum x1, waiting for transfers between devices, local_block(): full_out = lax.psum(part_out, 'tp')  1100 us
    all_to_all x1, blocking collectives, local_block(): recv_buf = lax.all_to_all(send_buf, 'ep', 0, 2, tiled=True)  743 us
    all_to_all x1, waiting for transfers between devices, local_block(): back_buf = lax.all_to_all(full_out, 'ep', 2, 0, tiled=True)  652 us
    gather x1, local copies, waits for them, and re-layouts, local_block(): back_buf[dest_pos].reshape(num_tok, top_k, model_dim).astype(jnp.float32)  191 us
    gather x1, local copies, waits for them, and re-layouts, local_block(): send_buf = normed[src_rows].reshape(ep_size, local_exp, slot_cap, model_dim)  124 us
    gather x5, local copies, waits for them, and re-layouts, route_local(): jnp.take_along_axis(logits, expert_ids, axis=1)  66.4 us
  transfers between devices with their start and end apart: 2, of which 2 were waited for; matrix products, arithmetic and copies ran while one was open for 2% of the time, Pallas kernels for 0%

commit v1 on v0

v1 whole, which is shorter than its diff:
```python
import functools

import jax
import jax.numpy as jnp
from jax import lax
from jax.experimental import pallas as pl
from jax.experimental.pallas import tpu as pltpu
from jax.sharding import PartitionSpec as P

NORM_EPS = 1e-5
NUM_CHUNKS = 2
ROW_TILE = 512
COL_TILE = 256


def route_dense(tokens, expert_ids, norm_gain, router_w):
    num_exp = router_w.shape[1]
    tok_f32 = tokens.astype(jnp.float32)
    inv_rms = lax.rsqrt(jnp.mean(tok_f32 * tok_f32, axis=-1, keepdims=True) + NORM_EPS)
    normed = (tok_f32 * inv_rms * norm_gain.astype(jnp.float32)).astype(jnp.bfloat16)
    logits = lax.dot_general(router_w, normed, (((0,), (1,)), ((), ())), preferred_element_type=jnp.float32)
    experts = jnp.arange(num_exp, dtype=jnp.int32)[:, None]
    ids = expert_ids.T
    chosen = functools.reduce(jnp.logical_or, [ids[k][None, :] == experts for k in range(ids.shape[0])])
    peak = jnp.max(jnp.where(chosen, logits, -jnp.inf), axis=0, keepdims=True)
    weight = jnp.where(chosen, jnp.exp(logits - peak), 0.0)
    return normed, weight / jnp.sum(weight, axis=0, keepdims=True)


def ffn_kernel(rows_ref, gate_ref, w1_ref, w3_ref, w2_ref, out_ref, hidden_ref, wide_ref):
    num_exp, width = w1_ref.shape[0], w1_ref.shape[2]
    tile = rows_ref.shape[0]
    for e in range(num_exp):
        wide_ref[e] = jnp.broadcast_to(gate_ref[:, e:e + 1], (tile, 128))

    def up(e, carry):
        rows = rows_ref[...]
        a = jnp.dot(rows, w1_ref[e], preferred_element_type=jnp.float32)
        b = jnp.dot(rows, w3_ref[e], preferred_element_type=jnp.float32)
        u = a * jax.nn.sigmoid(a) * b
        keep = jnp.concatenate([wide_ref[e]] * (width // 128), axis=1) > 0.0
        hidden_ref[e] = jnp.where(keep, u, 0.0).astype(jnp.bfloat16)
        return carry

    lax.fori_loop(0, num_exp, up, 0)

    def down(n, carry):
        cols = pl.ds(pl.multiple_of(n * COL_TILE, COL_TILE), COL_TILE)
        total = None
        for e in range(num_exp):
            y = jnp.dot(hidden_ref[e], w2_ref[e, :, cols], preferred_element_type=jnp.float32)
            term = jnp.concatenate([wide_ref[e]] * (COL_TILE // 128), axis=1) * y
            total = term if total is None else total + term
        out_ref[:, cols] = total
        return carry

    lax.fori_loop(0, out_ref.shape[1] // COL_TILE, down, 0)


def dense_experts(rows, gates, w_gate, w_up, w_down):
    num_rows, dim = rows.shape
    num_exp, _, width = w_gate.shape
    tile = min(ROW_TILE, num_rows)
    whole = lambda shape: pl.BlockSpec(shape, lambda i: (0,) * len(shape), pipeline_mode=pl.Buffered(1))
    return pl.pallas_call(
        ffn_kernel,
        out_shape=jax.ShapeDtypeStruct((num_rows, dim), jnp.float32),
        grid=(num_rows // tile,),
        in_specs=[pl.BlockSpec((tile, dim), lambda i: (i, 0)), pl.BlockSpec((tile, num_exp), lambda i: (i, 0)),
                  whole(w_gate.shape), whole(w_up.shape), whole(w_down.shape)],
        out_specs=pl.BlockSpec((tile, dim), lambda i: (i, 0)),
        scratch_shapes=[pltpu.VMEM((num_exp, tile, width), jnp.bfloat16), pltpu.VMEM((num_exp, tile, 128), jnp.float32)],
        compiler_params=pltpu.CompilerParams(dimension_semantics=("arbitrary",), vmem_limit_bytes=60 * 2**20),
        cost_estimate=pl.CostEstimate(flops=6 * num_rows * num_exp * dim * width, transcendentals=num_rows * num_exp * width,
                                      bytes_accessed=6 * num_rows * dim + 6 * num_exp * dim * width),
    )(rows, gates, w_gate, w_up, w_down)


def solution(mesh):
    ep_size, tp_size = mesh.shape['ep'], mesh.shape['tp']
    tok_spec = P(('dp', 'ep'), None)

    def local_block(tokens, expert_ids, norm_gain, router_w, w_gate, w_up, w_down):
        num_tok, dim = tokens.shape
        local_exp = w_gate.shape[0]
        normed, gates = route_dense(tokens, expert_ids, norm_gain, router_w)
        gates = lax.all_to_all(gates.reshape(ep_size, local_exp, num_tok), 'ep', 0, 0, tiled=True)
        gates = jnp.transpose(gates, (0, 2, 1))
        own_rows = num_tok // tp_size
        piece = own_rows // NUM_CHUNKS
        own_start = lax.axis_index('tp') * own_rows
        own_normed = lax.dynamic_slice_in_dim(normed, own_start, own_rows, 0)
        gates = gates.reshape(ep_size * tp_size, NUM_CHUNKS, piece, local_exp)
        mixed = []
        for c in range(NUM_CHUNKS):
            rows = lax.all_gather(own_normed[c * piece:(c + 1) * piece], ('ep', 'tp'), tiled=True)
            partial = dense_experts(rows, gates[:, c].reshape(rows.shape[0], local_exp), w_gate, w_up, w_down)
            mixed.append(lax.psum_scatter(partial, ('ep', 'tp'), scatter_dimension=0, tiled=True))
        own = lax.dynamic_slice_in_dim(tokens, own_start, own_rows, 0)
        done = (own.astype(jnp.float32) + jnp.concatenate(mixed, axis=0)).astype(jnp.bfloat16)
        return lax.all_gather(done, 'tp', tiled=True)

    return jax.shard_map(local_block, mesh=mesh, in_specs=(tok_spec, tok_spec, P(None), P(None, None), P('ep', None, 'tp'), P('ep', None, 'tp'), P('ep', 'tp', None)), out_specs=tok_spec, check_vma=False)
```

time: 3290 us -> 611 us (0.19)
  waiting for transfers between devices: 1750 us -> 267 us
  blocking collectives: 743 us -> 14.1 us
  local copies, waits for them, and re-layouts: 575 us -> 11 us
  Pallas kernels: 0 us -> 289 us
  matrix products: 102 us -> 3.68 us
  other arithmetic: 87.6 us -> 12 us
    psum x1 -> x0, waiting for transfers between devices: 1100 us -> none  [local_block(): full_out = lax.psum(part_out, 'tp')]
    all_to_all x1, blocking collectives: 743 us -> 14.1 us  [local_block(): lax.all_to_all(gates.reshape(ep_size, local_exp, num_tok), 'ep', 0, 0, ti...]
    all_to_all x1 -> x0, waiting for transfers between devices: 652 us -> none  [local_block(): back_buf = lax.all_to_all(full_out, 'ep', 2, 0, tiled=True)]
    gather x7 -> x0, local copies, waits for them, and re-layouts: 382 us -> none  [the longest x1 191 us: local_block(): back_buf[dest_pos].reshape(num_tok, top_k, model_dim).astype(jnp.float32)]
    pallas_call x0 -> x2, Pallas kernels: none -> 289 us  [dense_experts(): pl.pallas_call(ffn_kernel, out_shape=jax.ShapeDtypeStruct((num_rows, dim)...]
    reduce_scatter x0 -> x2, waiting for transfers between devices: none -> 169 us  [local_block(): lax.psum_scatter(partial, ('ep', 'tp'), scatter_dimension=0, tiled=True)]
    all_to_all x2 -> x0, local copies, waits for them, and re-layouts: 101 us -> none  [the longest x1 57.3 us: local_block(): back_buf = lax.all_to_all(full_out, 'ep', 2, 0, tiled=True)]
    dot_general x4 -> x1, matrix products: 102 us -> 3.68 us  [route_dense(): lax.dot_general(router_w, normed, (((0,), (1,)), ((), ())), preferred_ele...]
  transfers between devices with their start and end apart: 2 -> 5, of which waited for: 2 -> 4; matrix products, arithmetic and copies ran while one was open for 2% -> 1% of each run, Pallas kernels for 0% -> 47%
where the time goes in v1:
time: 611 us
  Pallas kernels  289 us (47%)
  waiting for transfers between devices  267 us (44%)
  blocking collectives  14.1 us (2%)
  between operations  13.3 us (2%)
  other arithmetic  12 us (2%)
  local copies, waits for them, and re-layouts  11 us (2%)
    pallas_call x2, Pallas kernels, dense_experts(): pl.pallas_call(ffn_kernel, out_shape=jax.ShapeDtypeStruct((num_rows, dim)...  289 us
    reduce_scatter x2, waiting for transfers between devices, local_block(): lax.psum_scatter(partial, ('ep', 'tp'), scatter_dimension=0, tiled=True)  169 us
    all_gather x2, waiting for transfers between devices, local_block(): lax.all_gather(own_normed[c * piece:(c + 1) * piece], ('ep', 'tp'), tiled...  52.3 us
    all_gather x1, waiting for transfers between devices, local_block(): return lax.all_gather(done, 'tp', tiled=True)  45.6 us
    all_to_all x1, blocking collectives, local_block(): lax.all_to_all(gates.reshape(ep_size, local_exp, num_tok), 'ep', 0, 0, ti...  14.1 us
  transfers between devices with their start and end apart: 5, of which 4 were waited for; matrix products, arithmetic and copies ran while one was open for 1% of the time, Pallas kernels for 47%

profile of v1, /device:TPU:97, one launch (start us, length us, event | category | flops | bytes accessed | tf_op | source)
XLA Modules:
  0.0 610.5 jit_solution(16155855364293040877)
XLA Ops:
  6.5 0.0 copy-start
  6.6 0.0 copy-start.3
  6.6 0.0 all-gather.4.cloned.1.call-start
  6.6 3.1 fusion
  9.7 0.0 copy-done.3
  9.7 0.0 copy-start.2
  9.7 5.2 fusion.2
  15.0 2.3 constant_dynamic-slice_fusion
  17.2 0.1 all-gather.4.cloned.1.call-update
  17.3 0.1 all-gather.6.cloned.1.call-start
  17.4 0.7 all-gather.6.cloned.1.call-update
  18.1 0.1 reduce-scatter.3.cloned.1.call-start
  18.2 0.0 copy-done.2
  18.2 0.0 copy-done
  18.2 3.7 select_reduce_fusion
  21.9 0.3 fusion.11
  22.2 0.2 divide_bitcast_fusion
  22.4 14.1 %all_to_all.5 = f32[8,8,1024]{2,1,0:T(8,128)S(1)} all-to-all(f32[8,8,1024]{2,1,0:T(8,128)S(1)} %divide_bitcast_fusion), channel_id=1, replica_groups=mesh['dp'=1,'tp'=4,'ep'=8] {'ep'}, dimensions={0} | all-to-all | bytes 524288 | tf_op jit(solution)/shard_map/all_to_all | solution.py:87
  36.5 1.9 copy.8
  38.5 52.3 %all-gather.4.cloned.1.call-done.rows_ref = bf16[4096,2048]{1,0:T(8,128)(2,1)} async-done(((bf16[128,2048]{1,0:T(8,128)(2,1)}), bf16[4096,2048]{1,0:T(8,128)(2,1)}) %all-gather.4.cloned.1.call-update) | async-done | bytes 16777232 | tf_op jit(solution)/shard_map/all_gather | solution.py:96
  90.8 144.4 %shard_map.73 = f32[4096,2048]{1,0:T(8,128)} custom-call(bf16[4096,2048]{1,0:T(8,128)(2,1)} %all-gather.4.cloned.1.call-done.rows_ref, f32[4096,8]{1,0:T(8,128)} %bitcast.20, bf16[8,2048,256]{2,1,0:T(8,128)(2,1)} %w1_ref.3, bf16[8,2048,256]{2,1,0:T(8,128)(2,1)} %w3_ref.3, bf16[8,256,2048]{2,1,0:T(8,128)(2,1)} %w2_ref.3), custom_call_target="tpu_custom_call" | custom-call | flops 103079215104 | bytes 75497472 | tf_op jit(solution)/shard_map/pallas_call | solution.py:65
  235.1 0.1 reduce-scatter.3.cloned.1.call-update
  235.2 0.1 reduce-scatter.5.cloned.1.call-start
  235.3 1.9 copy.9
  237.2 0.0 all-gather.6.cloned.1.call-done.rows_ref
  237.2 144.4 %shard_map.74 = f32[4096,2048]{1,0:T(8,128)} custom-call(bf16[4096,2048]{1,0:T(8,128)(2,1)} %all-gather.6.cloned.1.call-done.rows_ref, f32[4096,8]{1,0:T(8,128)} %bitcast.21, bf16[8,2048,256]{2,1,0:T(8,128)(2,1)} %w1_ref.3, bf16[8,2048,256]{2,1,0:T(8,128)(2,1)} %w3_ref.3, bf16[8,256,2048]{2,1,0:T(8,128)(2,1)} %w2_ref.3), custom_call_target="tpu_custom_call" | custom-call | flops 103079215104 | bytes 75497472 | tf_op jit(solution)/shard_map/pallas_call | solution.py:65
  381.6 0.1 reduce-scatter.5.cloned.1.call-update
  381.7 0.1 all-gather.8.cloned.1.call-start
  381.7 8.7 %reduce-scatter.3.cloned.1.call-done = f32[128,2048]{1,0:T(8,128)} async-done(((f32[4096,2048]{1,0:T(8,128)}), f32[128,2048]{1,0:T(8,128)}) %reduce-scatter.3.cloned.1.call-update) | async-done | bytes 1048592 | tf_op jit(solution)/shard_map/reduce_scatter | solution.py:98
  390.5 159.9 %reduce-scatter.5.cloned.1.call-done = f32[128,2048]{1,0:T(8,128)} async-done(((f32[4096,2048]{1,0:T(8,128)}), f32[128,2048]{1,0:T(8,128)}) %reduce-scatter.5.cloned.1.call-update) | async-done | bytes 1048592 | tf_op jit(solution)/shard_map/reduce_scatter | solution.py:98
  550.4 3.1 fusion.3
  553.5 0.1 all-gather.8.cloned.1.call-update
  553.5 0.0 copy-start.1
  553.5 45.6 %all-gather.8.cloned.1.call-done = bf16[1024,2048]{1,0:T(8,128)(2,1)} async-done(((bf16[256,2048]{1,0:T(8,128)(2,1)}), bf16[1024,2048]{1,0:T(8,128)(2,1)}) %all-gather.8.cloned.1.call-update) | async-done | bytes 4194320 | tf_op jit(solution)/shard_map/all_gather | solution.py:101
  599.2 4.8 copy.11
  604.0 0.0 copy-done.1
  (4 shorter events, 0.1 us)
Async XLA Ops:
  6.5 11.7 %copy-start = (bf16[2048,64]{0,1:T(8,128)(2,1)S(1)}, bf16[2048,64]{0,1:T(8,128)(2,1)}, u32[]{:S(2)}) copy-start(bf16[2048,64]{0,1:T(8,128)(2,1)} %param.10) | copy-start | bytes 786436
  6.6 3.1 copy-start.3
  6.6 84.2 %all-gather.4.cloned.1.call-start = ((), (), s32[]{:S(2)}) async-start(), calls=%async_computation.3 | async-start | bytes 17301504 | tf_op jit(solution)/shard_map/all_gather | solution.py:96
  9.7 8.4 %copy-start.2 = (s32[1024,8]{0,1:T(8,128)S(1)}, s32[1024,8]{0,1:T(8,128)}, u32[]{:S(2)}) copy-start(s32[1024,8]{0,1:T(8,128)} %param.8) | copy-start | bytes 98308
  17.3 219.9 %all-gather.6.cloned.1.call-start = ((), (), s32[]{:S(2)}) async-start(), calls=%async_computation.5 | async-start | bytes 17301504 | tf_op jit(solution)/shard_map/all_gather | solution.py:96
  18.1 372.4 %reduce-scatter.3.cloned.1.call-start = ((), (), s32[]{:S(2)}) async-start(), calls=%async_computation.4 | async-start | bytes 34603008 | tf_op jit(solution)/shard_map/reduce_scatter | solution.py:98
  235.2 315.2 %reduce-scatter.5.cloned.1.call-start = ((), (), s32[]{:S(2)}) async-start(), calls=%async_computation.6 | async-start | bytes 34603008 | tf_op jit(solution)/shard_map/reduce_scatter | solution.py:98
  381.7 217.5 %all-gather.8.cloned.1.call-start = ((), (), s32[]{:S(2)}) async-start(), calls=%async_computation.7 | async-start | bytes 5242880 | tf_op jit(solution)/shard_map/all_gather | solution.py:101
  553.5 50.4 %copy-start.1 = (bf16[2048,64]{0,1:T(8,128)(2,1)S(1)}, bf16[2048,64]{0,1:T(8,128)(2,1)}, u32[]{:S(2)}) copy-start(bf16[2048,64]{0,1:T(8,128)(2,1)} %param.10) | copy-start | bytes 786436
Sparse Core Ops, SparseCore 0:
  17.4 73.3 all-gather.3
  92.8 66.6 all-gather.5
  235.3 155.1 reduce-scatter.2
  394.1 156.2 reduce-scatter.4
  553.6 45.4 all-gather.7

commit v2 on v1

v2 whole, which is shorter than its diff:
```python
import functools

import jax
import jax.numpy as jnp
from jax import lax
from jax.experimental import pallas as pl
from jax.experimental.pallas import tpu as pltpu
from jax.sharding import PartitionSpec as P

NORM_EPS = 1e-5
COL_TILE = 256
PIECE = 16
RING = 4


def route_dense(tokens, expert_ids, norm_gain, router_w):
    num_exp = router_w.shape[1]
    tok_f32 = tokens.astype(jnp.float32)
    inv_rms = lax.rsqrt(jnp.mean(tok_f32 * tok_f32, axis=-1, keepdims=True) + NORM_EPS)
    normed = (tok_f32 * inv_rms * norm_gain.astype(jnp.float32)).astype(jnp.bfloat16)
    logits = lax.dot_general(router_w, normed, (((0,), (1,)), ((), ())), preferred_element_type=jnp.float32)
    experts = jnp.arange(num_exp, dtype=jnp.int32)[:, None]
    ids = expert_ids.T
    chosen = functools.reduce(jnp.logical_or, [ids[k][None, :] == experts for k in range(ids.shape[0])])
    peak = jnp.max(jnp.where(chosen, logits, -jnp.inf), axis=0, keepdims=True)
    weight = jnp.where(chosen, jnp.exp(logits - peak), 0.0)
    return normed, weight / jnp.sum(weight, axis=0, keepdims=True)


def moe_kernel(steps, keep, h_ref, tok_ref, gate_ref, w1_ref, w3_ref, w2_ref, out_ref, pool_ref,
               rows_buf, gate_buf, hidden_ref, wide_ref, mine, other, part, from_far, from_front, from_back, quarter, from_x,
               own_sem, own_front_send, own_back_send, relay_send, pair_send, back_recv, front_recv, far_recv, pair_recv,
               load_sem, sum_send, sum_recv, far_send, far_sum_recv, near_send, near_recv, relay_sum_send, relay_sum_recv, x_send, x_recv):
    num_exp, width = w1_ref.shape[0], w1_ref.shape[2]
    dim = h_ref.shape[2]
    ep, y = lax.axis_index("ep"), lax.axis_index("tp")
    x, core = ep // 2, ep % 2
    turn = 1 + 2 * core
    xf, xb, yf, yb = (x + turn) % RING, (x + RING - turn) % RING, (y + turn) % RING, (y + RING - turn) % RING
    xo, yo = (x + 2) % RING, (y + 2) % RING
    at_x = lambda other_x: {"ep": other_x * 2 + core}
    at_y = lambda other_y: {"tp": other_y}
    pair = {"ep": x * 2 + 1 - core}

    def remote(src, dst, send, recv, to):
        return pltpu.make_async_remote_copy(src_ref=src, dst_ref=dst, send_sem=send, recv_sem=recv, device_id=to, device_id_type=pl.DeviceIdType.MESH)

    barrier = pltpu.get_barrier_semaphore()
    peers = (pair, at_x(xf), at_x(xb), at_x(xo), at_y(yf), at_y(yb))
    for peer in peers:
        pl.semaphore_signal(barrier, inc=1, device_id=peer, device_id_type=pl.DeviceIdType.MESH)
    pl.semaphore_wait(barrier, len(peers))

    def within(chunk):
        return jnp.logical_and(chunk >= 0, chunk < steps)

    own_copy = lambda k: pltpu.make_async_copy(h_ref.at[k], pool_ref.at[k, core, x], own_sem.at[k])
    own_front = lambda k: remote(h_ref.at[k], pool_ref.at[k, core, x], own_front_send.at[k], back_recv.at[k], at_x(xf))
    own_back = lambda k: remote(h_ref.at[k], pool_ref.at[k, core, x], own_back_send.at[k], front_recv.at[k], at_x(xb))
    relay = lambda k: remote(pool_ref.at[k, core, xb], pool_ref.at[k, core, xb], relay_send.at[k], far_recv.at[k], at_x(xf))
    to_pair = lambda k: remote(pool_ref.at[k, core], pool_ref.at[k, core], pair_send.at[k], pair_recv.at[k], pair)

    def loads(k, slot):
        return [pltpu.make_async_copy(pool_ref.at[k, core], rows_buf.at[slot, 0], load_sem.at[slot, 0]),
                pltpu.make_async_copy(pool_ref.at[k, 1 - core], rows_buf.at[slot, 1], load_sem.at[slot, 1]),
                pltpu.make_async_copy(gate_ref.at[k, core], gate_buf.at[slot, 0], load_sem.at[slot, 2]),
                pltpu.make_async_copy(gate_ref.at[k, 1 - core], gate_buf.at[slot, 1], load_sem.at[slot, 3])]

    sum_copy = lambda k: remote(other, part.at[k % keep], sum_send, sum_recv.at[k % keep], pair)
    far_copy = lambda k: remote(part.at[k % keep, :, yo], from_far.at[k % keep], far_send, far_sum_recv.at[k % keep], at_y(yf))
    near_copy = lambda k: remote(part.at[k % keep, :, yb], from_front.at[k % keep], near_send, near_recv.at[k % keep], at_y(yb))
    next_copy = lambda k: remote(part.at[k % keep, :, yf], from_back.at[k % keep], relay_sum_send, relay_sum_recv.at[k % keep], at_y(yf))
    x_copies = lambda k: [remote(quarter.at[k % 2, (x + d) % RING], from_x.at[k % keep, d - 1], x_send.at[d - 1], x_recv.at[k % keep, d - 1],
                                 at_x((x + d) % RING)) for d in range(1, RING)]

    def gather_ahead(t):
        @pl.when(within(t + 4))
        def _():
            own_copy(t + 4).start()
            own_front(t + 4).start()
            own_back(t + 4).start()

        @pl.when(within(t + 3))
        def _():
            own_front(t + 3).wait_recv()
            relay(t + 3).start()

        @pl.when(within(t + 2))
        def _():
            own_back(t + 2).wait_recv()
            relay(t + 2).wait_recv()
            own_copy(t + 2).wait()
            to_pair(t + 2).start()

        @pl.when(within(t + 1))
        def _():
            to_pair(t + 1).wait_recv()
            for copy in loads(t + 1, (t + 1) % 2):
                copy.start()

    def experts(t):
        slot = t % 2
        for copy in loads(t, slot):
            copy.wait()
        half = wide_ref.shape[1] // 2
        for e in range(num_exp):
            for p in range(2):
                wide_ref[e, p * half:(p + 1) * half] = jnp.broadcast_to(gate_buf[slot, p, :, e:e + 1], (half, 128))

        def up(e, carry):
            rows = rows_buf[slot].reshape(2 * half, dim)
            a = jnp.dot(rows, w1_ref[e], preferred_element_type=jnp.float32)
            b = jnp.dot(rows, w3_ref[e], preferred_element_type=jnp.float32)
            u = a * jax.nn.sigmoid(a) * b
            chosen = jnp.concatenate([wide_ref[e]] * (width // 128), axis=1) > 0.0
            hidden_ref[e] = jnp.where(chosen, u, 0.0).astype(jnp.bfloat16)
            return carry

        lax.fori_loop(0, num_exp, up, 0)

        @pl.when(t >= 1)
        def _():
            sum_copy(t - 1).wait_send()

        def down(n, carry):
            cols = pl.ds(pl.multiple_of(n * COL_TILE, COL_TILE), COL_TILE)
            total = None
            for e in range(num_exp):
                term = jnp.concatenate([wide_ref[e]] * (COL_TILE // 128), axis=1) * jnp.dot(hidden_ref[e], w2_ref[e, :, cols], preferred_element_type=jnp.float32)
                total = term if total is None else total + term
            total = total.reshape((2,) + other.shape[:3] + (COL_TILE,))
            mine[slot, :, :, :, cols] = total[0]
            other[:, :, :, cols] = total[1]
            return carry

        lax.fori_loop(0, dim // COL_TILE, down, 0)

    def reduce_behind(t):
        @pl.when(within(t - 2))
        def _():
            far_copy(t - 2).wait_send()
            near_copy(t - 2).wait_send()

        @pl.when(within(t - 3))
        def _():
            next_copy(t - 3).wait_send()

        @pl.when(within(t - 4))
        def _():
            k = t - 4
            for copy in x_copies(k):
                copy.wait_send()
            for copy in x_copies(k):
                copy.wait_recv()
            mixed = quarter[k % 2, x] + from_x[k % keep, 0] + from_x[k % keep, 1] + from_x[k % keep, 2]
            out_ref[k] = (tok_ref[k].astype(jnp.float32) + mixed).astype(jnp.bfloat16)

        @pl.when(within(t - 3))
        def _():
            k = t - 3
            near_copy(k).wait_recv()
            next_copy(k).wait_recv()
            for i in range(RING):
                quarter[k % 2, i] = part[k % keep, i, y] + from_front[k % keep, i] + from_back[k % keep, i]
            for copy in x_copies(k):
                copy.start()

        @pl.when(within(t - 2))
        def _():
            k = t - 2
            far_copy(k).wait_recv()
            for i in range(RING):
                part[k % keep, i, yf] = part[k % keep, i, yf] + from_far[k % keep, i]
            next_copy(k).start()

        @pl.when(within(t - 1))
        def _():
            k = t - 1
            sum_copy(k).wait_recv()

            def add(i, carry):
                for q in range(RING):
                    part[k % keep, i, q] = part[k % keep, i, q] + mine[k % 2, i, q]
                return carry

            lax.fori_loop(0, RING, add, 0)
            far_copy(k).start()
            near_copy(k).start()

        @pl.when(within(t))
        def _():
            sum_copy(t).start()

    def step(i, carry):
        t = i - 4
        gather_ahead(t)
        pl.when(within(t))(lambda: experts(t))
        reduce_behind(t)
        return carry

    lax.fori_loop(0, steps + 8, step, 0)
    sum_copy(steps - 1).wait_send()

    def drain(k, carry):
        own_front(k).wait_send()
        own_back(k).wait_send()
        relay(k).wait_send()
        to_pair(k).wait_send()
        return carry

    lax.fori_loop(0, steps, drain, 0)


def fused_experts(h, tok, gates, w_gate, w_up, w_down):
    steps, rows, dim = h.shape
    num_exp, _, width = w_gate.shape
    piece, keep = rows // RING, 4
    chunk = 2 * RING * rows
    vmem = pl.BlockSpec(memory_space=pltpu.VMEM)
    hbm = pl.BlockSpec(memory_space=pl.ANY)
    quad = (RING, RING, piece, dim)
    dma = pltpu.SemaphoreType.DMA
    out, _ = pl.pallas_call(
        functools.partial(moe_kernel, steps, keep),
        out_shape=(jax.ShapeDtypeStruct((steps, piece, dim), jnp.bfloat16), jax.ShapeDtypeStruct((steps, 2, RING, rows, dim), jnp.bfloat16)),
        in_specs=[hbm, vmem, hbm, vmem, vmem, vmem],
        out_specs=(vmem, hbm),
        scratch_shapes=[
            pltpu.VMEM((2, 2, RING, rows, dim), jnp.bfloat16), pltpu.VMEM((2, 2, chunk // 2, num_exp), jnp.float32),
            pltpu.VMEM((num_exp, chunk, width), jnp.bfloat16), pltpu.VMEM((num_exp, chunk, 128), jnp.float32),
            pltpu.VMEM((2,) + quad, jnp.float32), pltpu.VMEM(quad, jnp.float32), pltpu.VMEM((keep,) + quad, jnp.float32),
            pltpu.VMEM((keep, RING, piece, dim), jnp.float32), pltpu.VMEM((keep, RING, piece, dim), jnp.float32),
            pltpu.VMEM((keep, RING, piece, dim), jnp.float32), pltpu.VMEM((2, RING, piece, dim), jnp.float32),
            pltpu.VMEM((keep, RING - 1, piece, dim), jnp.float32),
            dma((steps,)), dma((steps,)), dma((steps,)), dma((steps,)), dma((steps,)), dma((steps,)), dma((steps,)), dma((steps,)), dma((steps,)),
            dma((2, 4)), dma, dma((keep,)), dma, dma((keep,)), dma, dma((keep,)), dma, dma((keep,)), dma((RING - 1,)), dma((keep, RING - 1)),
        ],
        compiler_params=pltpu.CompilerParams(collective_id=0, has_side_effects=True, vmem_limit_bytes=67043328),
        cost_estimate=pl.CostEstimate(flops=6 * steps * chunk * num_exp * dim * width, transcendentals=steps * chunk * num_exp * width,
                                      bytes_accessed=2 * steps * chunk * dim + 6 * num_exp * dim * width),
    )(h, tok, gates, w_gate, w_up, w_down)
    return out


def solution(mesh):
    ep_size, tp_size = mesh.shape['ep'], mesh.shape['tp']
    tok_spec = P(('dp', 'ep'), None)

    def local_block(tokens, expert_ids, norm_gain, router_w, w_gate, w_up, w_down):
        num_tok, dim = tokens.shape
        local_exp = w_gate.shape[0]
        normed, gates = route_dense(tokens, expert_ids, norm_gain, router_w)
        own_rows = num_tok // tp_size
        steps = own_rows // PIECE
        gates = lax.all_to_all(gates.reshape(ep_size, local_exp, num_tok), 'ep', 0, 0, tiled=True)
        gates = gates.reshape(ep_size // 2, 2, local_exp, tp_size, steps, PIECE)
        gates = jnp.transpose(gates, (4, 1, 0, 3, 5, 2)).reshape(steps, 2, ep_size // 2 * tp_size * PIECE, local_exp)
        h = jnp.transpose(normed.reshape(tp_size, steps, PIECE, dim), (1, 0, 2, 3)).reshape(steps, tp_size * PIECE, dim)
        own = lax.dynamic_slice_in_dim(tokens, lax.axis_index('tp') * own_rows, own_rows, 0).reshape(steps, PIECE, dim)
        done = fused_experts(h, own, gates, w_gate, w_up, w_down)
        return lax.all_gather(done.reshape(own_rows, dim), 'tp', tiled=True)

    return jax.shard_map(local_block, mesh=mesh, in_specs=(tok_spec, tok_spec, P(None), P(None, None), P('ep', None, 'tp'), P('ep', None, 'tp'), P('ep', 'tp', None)), out_specs=tok_spec, check_vma=False)
```

time: 611 us -> 493 us (0.81)
  waiting for transfers between devices: 267 us -> 46 us
  Pallas kernels: 289 us -> 401 us
  blocking collectives: 14.1 us -> 0 us
  local copies, waits for them, and re-layouts: 11 us -> 18.5 us
  other arithmetic: 12 us -> 5.45 us
    reduce_scatter x2 -> x0, waiting for transfers between devices: 169 us -> none  [local_block(): lax.psum_scatter(partial, ('ep', 'tp'), scatter_dimension=0, tiled=True)]
    pallas_call x2 -> x1, Pallas kernels: 289 us -> 401 us  [fused_experts(): pl.pallas_call(functools.partial(moe_kernel, steps, keep), out_shape=(jax...]
    all_gather x3 -> x1, waiting for transfers between devices: 97.9 us -> 45.9 us  [local_block(): return lax.all_gather(done.reshape(own_rows, dim), 'tp', tiled=True)]
    all_to_all x1 -> x0, blocking collectives: 14.1 us -> none  [local_block(): lax.all_to_all(gates.reshape(ep_size, local_exp, num_tok), 'ep', 0, 0, ti...]
    slice x4 -> x0, local copies, waits for them, and re-layouts: 6.14 us -> none  [the longest x3 3.88 us: local_block(): gates[:, c].reshape(rows.shape[0], local_exp)]
  transfers between devices with their start and end apart: 5 -> 2, of which waited for: 4 -> 1; matrix products, arithmetic and copies ran while one was open for 1% -> 1% of each run, Pallas kernels for 47% -> 0%
where the time goes in v2:
time: 493 us; the launch traced here: 492 us
  Pallas kernels  401 us (81%)
  waiting for transfers between devices  46 us (9%)
  local copies, waits for them, and re-layouts  18.5 us (4%)
  between operations  13.5 us (3%)
  starting transfers between devices  6.02 us (1%)
  other arithmetic  5.45 us (1%)
    pallas_call x1, Pallas kernels, fused_experts(): pl.pallas_call(functools.partial(moe_kernel, steps, keep), out_shape=(jax...  401 us
    all_gather x1, waiting for transfers between devices, local_block(): return lax.all_gather(done.reshape(own_rows, dim), 'tp', tiled=True)  45.9 us
  transfers between devices with their start and end apart: 2, of which 1 were waited for; matrix products, arithmetic and copies ran while one was open for 1% of the time, Pallas kernels for 0%

profile of v2, /device:TPU:97, one launch (start us, length us, event | category | flops | bytes accessed | tf_op | source)
XLA Modules:
  0.0 492.4 jit_solution(2625873689516807516)
XLA Ops:
  6.5 0.0 copy-start
  6.5 0.0 copy-start.2
  6.6 3.2 fusion
  9.8 0.0 copy-done.2
  9.8 1.1 fusion.11
  10.9 0.0 copy-done
  10.9 0.0 copy-start.3
  10.9 1.0 fusion.2
  12.0 0.0 copy-start.1
  12.0 2.0 copy-done.1
  14.0 0.0 copy-done.3
  14.0 1.5 select_reduce_fusion
  15.5 0.3 fusion.10
  15.7 0.9 divide_bitcast_fusion
  16.7 6.0 %all-to-all-start = ((f32[8,8,1024]{2,1,0:T(8,128)}), f32[8,8,1024]{2,1,0:T(8,128)S(1)}, u32[]{:S(2)}, u32[]{:S(2)}) async-start(f32[8,8,1024]{2,1,0:T(8,128)} %divide_bitcast_fusion), calls=%async_computation | async-start | bytes 524288 | tf_op jit(solution)/shard_map/all_to_all | solution.py:255
  22.7 0.0 all-gather.2.cloned.1.call-start
  22.7 4.8 copy.9
  27.5 2.3 constant_dynamic-slice_fusion
  29.8 0.0 all-to-all-done
  29.8 0.7 reshape.36
  30.5 2.8 copy.10
  33.3 401.4 %shard_map.73 = (bf16[16,16,2048]{2,1,0:T(8,128)(2,1)}, bf16[16,2,4,64,2048]{4,3,2,1,0:T(8,128)(2,1)}) custom-call(bf16[16,64,2048]{2,1,0:T(8,128)(2,1)} %bitcast.26, bf16[16,16,2048]{2,1,0:T(8,128)(2,1)} %bitcast.27, f32[16,2,256,8]{3,2,1,0:T(8,128)} %bitcast.25, bf16[8,2048,256]{2,1,0:T(8,128)(2,1)} %w1_ref.1, bf16[8,2048,256]{2,1,0:T(8,128)(2,1)} %w3_ref.1, ...), custom_call_target="tpu_custom_call" | custom-call | flops 206158430208 | bytes 58720256 | tf_op jit(solution)/shard_map/pallas_call | solution.py:223
  434.8 0.1 all-gather.2.cloned.1.call-update
  434.8 45.9 %all-gather.2.cloned.1.call-done = bf16[1024,2048]{1,0:T(8,128)(2,1)} async-done(((bf16[256,2048]{1,0:T(8,128)(2,1)}), bf16[1024,2048]{1,0:T(8,128)(2,1)}) %all-gather.2.cloned.1.call-update) | async-done | bytes 4194320 | tf_op jit(solution)/shard_map/all_gather | solution.py:261
  480.8 4.8 copy.12
  (2 shorter events, 0.0 us)
Async XLA Ops:
  6.5 4.4 copy-start
  6.5 3.3 copy-start.2
  10.9 3.1 copy-start.3
  12.0 2.0 copy-start.1
  16.7 13.1 %all-to-all-start = ((f32[8,8,1024]{2,1,0:T(8,128)}), f32[8,8,1024]{2,1,0:T(8,128)S(1)}, u32[]{:S(2)}, u32[]{:S(2)}) async-start(f32[8,8,1024]{2,1,0:T(8,128)} %divide_bitcast_fusion), calls=%async_computation | async-start | bytes 524288 | tf_op jit(solution)/shard_map/all_to_all | solution.py:255
  22.7 458.1 %all-gather.2.cloned.1.call-start = ((), (), s32[]{:S(2)}) async-start(), calls=%async_computation.1 | async-start | bytes 5242880 | tf_op jit(solution)/shard_map/all_gather | solution.py:261
Sparse Core Ops, SparseCore 0:
  434.9 45.7 all-gather.1

commit v3 on v2

--- a/solution.py
+++ b/solution.py
@@ -11,6 +11,7 @@
 COL_TILE = 256
 PIECE = 16
 RING = 4
+KEEP = 5
 
 
 def route_dense(tokens, expert_ids, norm_gain, router_w):
@@ -27,12 +28,13 @@
     return normed, weight / jnp.sum(weight, axis=0, keepdims=True)
 
 
-def moe_kernel(steps, keep, h_ref, tok_ref, gate_ref, w1_ref, w3_ref, w2_ref, out_ref, pool_ref,
-               rows_buf, gate_buf, hidden_ref, wide_ref, mine, other, part, from_far, from_front, from_back, quarter, from_x,
+def moe_kernel(steps, keep, h_ref, tok_ref, gate_ref, w1_hbm, w3_hbm, w2_hbm, out_ref, pool_ref,
+               w1_ref, w3_ref, w2_ref, out_buf, rows_buf, gate_buf, hidden_ref, wide_ref, mine, other, part, from_far, from_front, from_back, quarter, from_x,
                own_sem, own_front_send, own_back_send, relay_send, pair_send, back_recv, front_recv, far_recv, pair_recv,
-               load_sem, sum_send, sum_recv, far_send, far_sum_recv, near_send, near_recv, relay_sum_send, relay_sum_recv, x_send, x_recv):
+               load_sem, sum_send, sum_recv, far_send, far_sum_recv, near_send, near_recv, relay_sum_send, relay_sum_recv, x_send, x_recv,
+               weight_sem, out_sem, out_front_send, out_back_send, out_relay_send, out_back_recv, out_front_recv, out_far_recv):
     num_exp, width = w1_ref.shape[0], w1_ref.shape[2]
-    dim = h_ref.shape[2]
+    dim = h_ref.shape[3]
     ep, y = lax.axis_index("ep"), lax.axis_index("tp")
     x, core = ep // 2, ep % 2
     turn = 1 + 2 * core
@@ -54,9 +56,9 @@
     def within(chunk):
         return jnp.logical_and(chunk >= 0, chunk < steps)
 
-    own_copy = lambda k: pltpu.make_async_copy(h_ref.at[k], pool_ref.at[k, core, x], own_sem.at[k])
-    own_front = lambda k: remote(h_ref.at[k], pool_ref.at[k, core, x], own_front_send.at[k], back_recv.at[k], at_x(xf))
-    own_back = lambda k: remote(h_ref.at[k], pool_ref.at[k, core, x], own_back_send.at[k], front_recv.at[k], at_x(xb))
+    own_copy = lambda k: pltpu.make_async_copy(h_ref.at[:, k], pool_ref.at[k, core, x], own_sem.at[k])
+    own_front = lambda k: remote(h_ref.at[:, k], pool_ref.at[k, core, x], own_front_send.at[k], back_recv.at[k], at_x(xf))
+    own_back = lambda k: remote(h_ref.at[:, k], pool_ref.at[k, core, x], own_back_send.at[k], front_recv.at[k], at_x(xb))
     relay = lambda k: remote(pool_ref.at[k, core, xb], pool_ref.at[k, core, xb], relay_send.at[k], far_recv.at[k], at_x(xf))
     to_pair = lambda k: remote(pool_ref.at[k, core], pool_ref.at[k, core], pair_send.at[k], pair_recv.at[k], pair)
 
@@ -66,12 +68,25 @@
                 pltpu.make_async_copy(gate_ref.at[k, core], gate_buf.at[slot, 0], load_sem.at[slot, 2]),
                 pltpu.make_async_copy(gate_ref.at[k, 1 - core], gate_buf.at[slot, 1], load_sem.at[slot, 3])]
 
+    weights = [pltpu.make_async_copy(src, dst, weight_sem.at[i]) for i, (src, dst) in enumerate(((w1_hbm, w1_ref), (w3_hbm, w3_ref), (w2_hbm, w2_ref)))]
+    for copy in weights:
+        copy.start()
+
     sum_copy = lambda k: remote(other, part.at[k % keep], sum_send, sum_recv.at[k % keep], pair)
-    far_copy = lambda k: remote(part.at[k % keep, :, yo], from_far.at[k % keep], far_send, far_sum_recv.at[k % keep], at_y(yf))
-    near_copy = lambda k: remote(part.at[k % keep, :, yb], from_front.at[k % keep], near_send, near_recv.at[k % keep], at_y(yb))
-    next_copy = lambda k: remote(part.at[k % keep, :, yf], from_back.at[k % keep], relay_sum_send, relay_sum_recv.at[k % keep], at_y(yf))
-    x_copies = lambda k: [remote(quarter.at[k % 2, (x + d) % RING], from_x.at[k % keep, d - 1], x_send.at[d - 1], x_recv.at[k % keep, d - 1],
-                                 at_x((x + d) % RING)) for d in range(1, RING)]
+
+    def reduce_copies(k):
+        slot = k % keep
+        far = remote(part.at[slot, :, yo], from_far.at[slot], far_send, far_sum_recv.at[slot], at_y(yf))
+        near = remote(part.at[slot, :, yb], from_front.at[slot], near_send, near_recv.at[slot], at_y(yb))
+        onward = remote(part.at[slot, :, yf], from_back.at[slot], relay_sum_send, relay_sum_recv.at[slot], at_y(yf))
+        direct = [remote(quarter.at[k % 2, (x + d) % RING], from_x.at[slot, d - 1], x_send.at[d - 1], x_recv.at[slot, d - 1],
+                         at_x((x + d) % RING)) for d in range(1, RING)]
+        return far, near, onward, direct
+
+    out_copy = lambda k: pltpu.make_async_copy(out_buf.at[k % 2], out_ref.at[y, k], out_sem.at[k % 2])
+    out_front = lambda k: remote(out_buf.at[k % 2], out_ref.at[y, k], out_front_send.at[k % 2], out_back_recv.at[k], at_y(yf))
+    out_back = lambda k: remote(out_buf.at[k % 2], out_ref.at[y, k], out_back_send.at[k % 2], out_front_recv.at[k], at_y(yb))
+    out_relay = lambda k: remote(out_ref.at[yb, k], out_ref.at[yb, k], out_relay_send.at[k], out_far_recv.at[k], at_y(yf))
 
     def gather_ahead(t):
         @pl.when(within(t + 4))
@@ -98,10 +113,16 @@
             for copy in loads(t + 1, (t + 1) % 2):
                 copy.start()
 
-    def experts(t):
+    def experts_up(t):
         slot = t % 2
         for copy in loads(t, slot):
             copy.wait()
+
+        @pl.when(t == 0)
+        def _():
+            for copy in weights:
+                copy.wait()
+
         half = wide_ref.shape[1] // 2
         for e in range(num_exp):
             for p in range(2):
@@ -116,7 +137,10 @@
             hidden_ref[e] = jnp.where(chosen, u, 0.0).astype(jnp.bfloat16)
             return carry
 
-        lax.fori_loop(0, num_exp, up, 0)
+        lax.fori_loop(0, num_exp, up, 0, unroll=8)
+
+    def experts_down(t):
+        slot = t % 2
 
         @pl.when(t >= 1)
         def _():
@@ -133,45 +157,72 @@
             other[:, :, :, cols] = total[1]
             return carry
 
-        lax.fori_loop(0, dim // COL_TILE, down, 0)
+        lax.fori_loop(0, dim // COL_TILE, down, 0, unroll=2)
+
+    def if_within(chunk, body):
+        pl.when(within(chunk))(lambda: body(chunk))
+
+    def reduce_between(t):
+        def sent_onward(k):
+            reduce_copies(k)[2].wait_send()
+
+        def pass_on(k):
+            far, _, onward, _ = reduce_copies(k)
+            far.wait_recv()
+            for i in range(RING):
+                part[k % keep, i, yf] = part[k % keep, i, yf] + from_far[k % keep, i]
+            onward.start()
+
+        if_within(t - 4, sent_onward)
+        if_within(t - 3, pass_on)
 
     def reduce_behind(t):
-        @pl.when(within(t - 2))
-        def _():
-            far_copy(t - 2).wait_send()
-            near_copy(t - 2).wait_send()
-
-        @pl.when(within(t - 3))
-        def _():
-            next_copy(t - 3).wait_send()
-
-        @pl.when(within(t - 4))
-        def _():
-            k = t - 4
-            for copy in x_copies(k):
+        def sent_first(k):
+            far, near, _, _ = reduce_copies(k)
+            far.wait_send()
+            near.wait_send()
+
+        def finish(k):
+            direct = reduce_copies(k)[3]
+            for copy in direct:
                 copy.wait_send()
-            for copy in x_copies(k):
+            for copy in direct:
                 copy.wait_recv()
             mixed = quarter[k % 2, x] + from_x[k % keep, 0] + from_x[k % keep, 1] + from_x[k % keep, 2]
-            out_ref[k] = (tok_ref[k].astype(jnp.float32) + mixed).astype(jnp.bfloat16)
-
-        @pl.when(within(t - 3))
-        def _():
-            k = t - 3
-            near_copy(k).wait_recv()
-            next_copy(k).wait_recv()
+            out_buf[k % 2] = (tok_ref[k].astype(jnp.float32) + mixed).astype(jnp.bfloat16)
+            out_copy(k).start()
+            out_front(k).start()
+            out_back(k).start()
+
+        def spread(k):
+            _, near, onward, direct = reduce_copies(k)
+            near.wait_recv()
+            onward.wait_recv()
             for i in range(RING):
                 quarter[k % 2, i] = part[k % keep, i, y] + from_front[k % keep, i] + from_back[k % keep, i]
-            for copy in x_copies(k):
+            for copy in direct:
                 copy.start()
 
-        @pl.when(within(t - 2))
-        def _():
-            k = t - 2
-            far_copy(k).wait_recv()
-            for i in range(RING):
-                part[k % keep, i, yf] = part[k % keep, i, yf] + from_far[k % keep, i]
-            next_copy(k).start()
+        def begin(k):
+            far, near, _, _ = reduce_copies(k)
+            far.start()
+            near.start()
+
+        if_within(t - 2, sent_first)
+
+        @pl.when(within(t - 7))
+        def _():
+            out_copy(t - 7).wait()
+            out_front(t - 7).wait_send()
+            out_back(t - 7).wait_send()
+
+        @pl.when(within(t - 6))
+        def _():
+            out_front(t - 6).wait_recv()
+            out_relay(t - 6).start()
+
+        if_within(t - 5, finish)
+        if_within(t - 4, spread)
 
         @pl.when(within(t - 1))
         def _():
@@ -184,8 +235,8 @@
                 return carry
 
             lax.fori_loop(0, RING, add, 0)
-            far_copy(k).start()
-            near_copy(k).start()
+
+        if_within(t - 1, begin)
 
         @pl.when(within(t))
         def _():
@@ -194,11 +245,13 @@
     def step(i, carry):
         t = i - 4
         gather_ahead(t)
-        pl.when(within(t))(lambda: experts(t))
+        pl.when(within(t))(lambda: experts_up(t))
+        reduce_between(t)
+        pl.when(within(t))(lambda: experts_down(t))
         reduce_behind(t)
         return carry
 
-    lax.fori_loop(0, steps + 8, step, 0)
+    lax.fori_loop(0, steps + 12, step, 0)
     sum_copy(steps - 1).wait_send()
 
     def drain(k, carry):
@@ -206,27 +259,32 @@
         own_back(k).wait_send()
         relay(k).wait_send()
         to_pair(k).wait_send()
+        out_relay(k).wait_send()
+        out_back(k).wait_recv()
+        out_relay(k).wait_recv()
         return carry
 
     lax.fori_loop(0, steps, drain, 0)
 
 
 def fused_experts(h, tok, gates, w_gate, w_up, w_down):
-    steps, rows, dim = h.shape
+    _, steps, piece, dim = h.shape
     num_exp, _, width = w_gate.shape
-    piece, keep = rows // RING, 4
-    chunk = 2 * RING * rows
+    keep = KEEP
+    chunk = 2 * RING * RING * piece
     vmem = pl.BlockSpec(memory_space=pltpu.VMEM)
     hbm = pl.BlockSpec(memory_space=pl.ANY)
     quad = (RING, RING, piece, dim)
     dma = pltpu.SemaphoreType.DMA
     out, _ = pl.pallas_call(
         functools.partial(moe_kernel, steps, keep),
-        out_shape=(jax.ShapeDtypeStruct((steps, piece, dim), jnp.bfloat16), jax.ShapeDtypeStruct((steps, 2, RING, rows, dim), jnp.bfloat16)),
-        in_specs=[hbm, vmem, hbm, vmem, vmem, vmem],
-        out_specs=(vmem, hbm),
+        out_shape=(jax.ShapeDtypeStruct((RING, steps, piece, dim), jnp.bfloat16), jax.ShapeDtypeStruct((steps, 2) + quad, jnp.bfloat16)),
+        in_specs=[hbm, vmem, hbm, hbm, hbm, hbm],
+        out_specs=(hbm, hbm),
         scratch_shapes=[
-            pltpu.VMEM((2, 2, RING, rows, dim), jnp.bfloat16), pltpu.VMEM((2, 2, chunk // 2, num_exp), jnp.float32),
+            pltpu.VMEM(w_gate.shape, w_gate.dtype), pltpu.VMEM(w_up.shape, w_up.dtype), pltpu.VMEM(w_down.shape, w_down.dtype),
+            pltpu.VMEM((2, piece, dim), jnp.bfloat16),
+            pltpu.VMEM((2, 2) + quad, jnp.bfloat16), pltpu.VMEM((2, 2, chunk // 2, num_exp), jnp.float32),
             pltpu.VMEM((num_exp, chunk, width), jnp.bfloat16), pltpu.VMEM((num_exp, chunk, 128), jnp.float32),
             pltpu.VMEM((2,) + quad, jnp.float32), pltpu.VMEM(quad, jnp.float32), pltpu.VMEM((keep,) + quad, jnp.float32),
             pltpu.VMEM((keep, RING, piece, dim), jnp.float32), pltpu.VMEM((keep, RING, piece, dim), jnp.float32),
@@ -234,6 +292,7 @@
             pltpu.VMEM((keep, RING - 1, piece, dim), jnp.float32),
             dma((steps,)), dma((steps,)), dma((steps,)), dma((steps,)), dma((steps,)), dma((steps,)), dma((steps,)), dma((steps,)), dma((steps,)),
             dma((2, 4)), dma, dma((keep,)), dma, dma((keep,)), dma, dma((keep,)), dma, dma((keep,)), dma((RING - 1,)), dma((keep, RING - 1)),
+            dma((3,)), dma((2,)), dma((2,)), dma((2,)), dma((steps,)), dma((steps,)), dma((steps,)), dma((steps,)),
         ],
         compiler_params=pltpu.CompilerParams(collective_id=0, has_side_effects=True, vmem_limit_bytes=67043328),
         cost_estimate=pl.CostEstimate(flops=6 * steps * chunk * num_exp * dim * width, transcendentals=steps * chunk * num_exp * width,
@@ -255,9 +314,9 @@
         gates = lax.all_to_all(gates.reshape(ep_size, local_exp, num_tok), 'ep', 0, 0, tiled=True)
         gates = gates.reshape(ep_size // 2, 2, local_exp, tp_size, steps, PIECE)
         gates = jnp.transpose(gates, (4, 1, 0, 3, 5, 2)).reshape(steps, 2, ep_size // 2 * tp_size * PIECE, local_exp)
-        h = jnp.transpose(normed.reshape(tp_size, steps, PIECE, dim), (1, 0, 2, 3)).reshape(steps, tp_size * PIECE, dim)
+        h = normed.reshape(tp_size, steps, PIECE, dim)
         own = lax.dynamic_slice_in_dim(tokens, lax.axis_index('tp') * own_rows, own_rows, 0).reshape(steps, PIECE, dim)
         done = fused_experts(h, own, gates, w_gate, w_up, w_down)
-        return lax.all_gather(done.reshape(own_rows, dim), 'tp', tiled=True)
+        return done.reshape(num_tok, dim)
 
     return jax.shard_map(local_block, mesh=mesh, in_specs=(tok_spec, tok_spec, P(None), P(None, None), P('ep', None, 'tp'), P('ep', None, 'tp'), P('ep', 'tp', None)), out_specs=tok_spec, check_vma=False)

time: 493 us -> 422 us (0.86)
  waiting for transfers between devices: 46 us -> 3.98 us
  between operations: 13.5 us -> 0.08 us
  Pallas kernels: 401 us -> 390 us
    all_gather x1 -> x0, waiting for transfers between devices: 45.9 us -> none  [local_block(): return lax.all_gather(done.reshape(own_rows, dim), 'tp', tiled=True)]
    pallas_call x1, Pallas kernels: 401 us -> 390 us  [fused_experts(): pl.pallas_call(functools.partial(moe_kernel, steps, keep), out_shape=(jax...]
  transfers between devices with their start and end apart: 2 -> 1, of which waited for: 1 -> 1; matrix products, arithmetic and copies ran while one was open for 1% -> 1% of each run, Pallas kernels for 0% -> 0%
where the time goes in v3:
time: 422 us; the launch traced here: 420 us
  Pallas kernels  390 us (92%)
  local copies, waits for them, and re-layouts  13.8 us (3%)
  starting transfers between devices  6.01 us (1%)
  other arithmetic  5.45 us (1%)
    pallas_call x1, Pallas kernels, fused_experts(): pl.pallas_call(functools.partial(moe_kernel, steps, keep), out_shape=(jax...  390 us
  transfers between devices with their start and end apart: 1, of which 1 were waited for; matrix products, arithmetic and copies ran while one was open for 1% of the time, Pallas kernels for 0%

profile of v3, /device:TPU:97, one launch (start us, length us, event | category | flops | bytes accessed | tf_op | source)
XLA Modules:
  0.0 420.3 jit_solution(12011838154793255774)
XLA Ops:
  0.0 0.0 copy-start
  0.0 0.0 copy-start.2
  0.0 3.2 fusion
  3.3 0.0 copy-done.2
  3.3 1.1 fusion.11
  4.4 0.0 copy-done
  4.4 0.0 copy-start.3
  4.4 1.0 fusion.2
  5.4 0.0 copy-start.1
  5.4 2.0 copy-done.1
  7.4 0.0 copy-done.3
  7.4 1.5 select_reduce_fusion
  8.9 0.3 fusion.10
  9.2 0.9 divide_bitcast_fusion
  10.1 6.0 %all-to-all-start = ((f32[8,8,1024]{2,1,0:T(8,128)}), f32[8,8,1024]{2,1,0:T(8,128)S(1)}, u32[]{:S(2)}, u32[]{:S(2)}) async-start(f32[8,8,1024]{2,1,0:T(8,128)} %divide_bitcast_fusion), calls=%async_computation | async-start | bytes 524288 | tf_op jit(solution)/shard_map/all_to_all | solution.py:314
  16.1 2.3 constant_dynamic-slice_fusion
  18.4 4.0 all-to-all-done
  22.4 0.7 reshape.32
  23.1 2.9 copy.8
  26.0 389.5 %shard_map.73 = (bf16[4,16,16,2048]{3,2,1,0:T(8,128)(2,1)}, bf16[16,2,4,4,16,2048]{5,4,3,2,1,0:T(8,128)(2,1)}) custom-call(bf16[4,16,16,2048]{3,2,1,0:T(8,128)(2,1)} %bitcast.22, bf16[16,16,2048]{2,1,0:T(8,128)(2,1)} %bitcast.24, f32[16,2,256,8]{3,2,1,0:T(8,128)} %bitcast.21, bf16[8,2048,256]{2,1,0:T(8,128)(2,1)} %w1_hbm.1, bf16[8,2048,256]{2,1,0:T(8,128)(2,1)} %w3_hbm.1, ...), custom_call_target="tpu_custom_call" | custom-call | flops 206158430208 | bytes 58720256 | tf_op jit(solution)/shard_map/pallas_call | solution.py:279
  415.5 4.8 %copy.10 = bf16[1024,2048]{1,0:T(8,128)(2,1)} copy(bf16[1024,2048]{1,0:T(8,128)(2,1)} %bitcast.23) | data formatting | bytes 8388608
  (2 shorter events, 0.0 us)
Async XLA Ops:
  0.0 4.4 %copy-start = (bf16[1024,2048]{1,0:T(8,128)(2,1)S(1)}, bf16[1024,2048]{1,0:T(8,128)(2,1)}, u32[]{:S(2)}) copy-start(bf16[1024,2048]{1,0:T(8,128)(2,1)} %param.7) | copy-start | bytes 12582916
  0.0 3.3 copy-start.2
  4.4 3.1 copy-start.3
  5.4 2.0 copy-start.1
  10.1 12.3 %all-to-all-start = ((f32[8,8,1024]{2,1,0:T(8,128)}), f32[8,8,1024]{2,1,0:T(8,128)S(1)}, u32[]{:S(2)}, u32[]{:S(2)}) async-start(f32[8,8,1024]{2,1,0:T(8,128)} %divide_bitcast_fusion), calls=%async_computation | async-start | bytes 524288 | tf_op jit(solution)/shard_map/all_to_all | solution.py:314
